TPU v7x, 32 devices: a whole 2x2x4 slice. The times are simulated.
32 devices in a mesh: groups: 2 (over y), seq: 4 (over z), head: 4 (over x, core).
Axes of the slice: x: 2, y: 2, z: 4, core: 2. Of those that a mesh axis runs over, the one named last changes fastest.
Arguments:
- residual: bfloat16 [4096, 2560], P(('groups', 'seq'), 'head'), parts along dimension 0, may hold values from -6 to 6
- x_in: bfloat16 [4096, 5120], P(('groups', 'seq'), 'head'), parts along dimension 0, may hold values from -6 to 6
- bc_in: bfloat16 [4096, 256], P(('groups', 'seq')), parts along dimension 0, may hold values from -1.5 to 1.5
- z_in: bfloat16 [4096, 5120], P(('groups', 'seq'), 'head'), parts along dimension 0, may hold values from -6 to 6
- dt_raw: float32 [80, 4096], P('head', ('groups', 'seq')), parts along dimension 1, may hold values from -5 to 5
- dt_bias: float32 [80], P('head'), may hold values from -3 to 0
- decay_rate: float32 [80], P('head'), may hold values from 0.0003 to 0.15
- d_skip: float32 [80], P('head'), may hold values from 1 to 4
- conv_x_weight: bfloat16 [4, 5120], P(None, 'head'), may hold values from -3 to 3
- conv_x_bias: bfloat16 [5120], P('head'), may hold values from -3 to 3
- conv_bc_weight: bfloat16 [4, 256], replicated, may hold values from -3 to 3
- conv_bc_bias: bfloat16 [256], replicated, may hold values from -3 to 3
- norm_gain: bfloat16 [5120], P('head'), may hold values from 0.5 to 1.5
- out_weight: bfloat16 [5120, 2560], P('head'), may hold values from -0.078125 to 0.078125
- final_gain: bfloat16 [2560], replicated, may hold values from 0.5 to 1.5
- lm_weight: bfloat16 [2560, 25600], P('seq', 'head'), may hold values from -15.811388 to 15.811388
- targets: int32 [4096], P(('groups', 'seq')), parts along dimension 0, may hold values from 0 to 25599
- doc_lengths: int32 [8], P('groups'), parts along dimension 0, may hold values from 1 to 1536, as said below
Outputs:
- block_out: bfloat16 [4096, 2560], P(('groups', 'seq'), 'head'), parts along dimension 0
- doc_loss: float32 [8], P('groups'), parts along dimension 0
There are 2 independent parts, one for each index of `groups`. A program takes and returns all parts, laid end to end along the dimension named above; an argument that names none is the same for every part. Nothing has to cross between parts.
Inputs may be any that keep to these rules, and one draw needn't show every extreme that they name: `doc_lengths`: the lengths of a group's 4 documents, in the order in which they are packed into its 2048 tokens; they sum to 2048.
All inputs are finite; a program needn't handle non-finite values.
Results may differ from a plain program's by a relative error of at most 0.00145.
The roundings to bfloat16 on the way count: a program that leaves them out, or rounds other values in their place, can miss the bound.
Values may be sent and summed in bfloat16 or wider, within the bound.
A program may use at most 128 MiB of HBM per device.

v0:
```python
import jax
import jax.numpy as jnp
from jax import lax
from jax.sharding import PartitionSpec as P

D = 2560
HEAD_SIZE = 64
STATE = 128
KERNEL = 4
SPAN = 256
INNER = 5120
EPSILON = 1e-05
HIGH = lax.Precision.HIGHEST


def shifted(array, axis, by):
    length = lax.axis_size(axis)
    pairs = [(i, i + by) for i in range(length) if 0 <= i + by < length]
    return lax.ppermute(array, axis, pairs)


def entering(part, axis, combine, identity):
    place = lax.axis_index(axis)
    gathered = jax.tree.map(lambda a: lax.all_gather(a, axis), part)
    state = jax.tree.map(lambda a, e: jnp.zeros_like(a) + jnp.asarray(e, a.dtype), part, identity)

    def one(lap, state):
        return combine(
            state, jax.tree.map(lambda a: lax.dynamic_index_in_dim(a, lap, 0, False), gathered)
        )

    return lax.fori_loop(0, place, one, state)


def merged(value, axis, join):
    pieces = jax.tree.map(lambda part: lax.all_gather(part, axis), value)
    head = jax.tree.map(lambda part: part[0], pieces)
    tail = jax.tree.map(lambda part: part[1:], pieces)
    running, _ = lax.scan(lambda running, section: (join(running, section), None), head, tail)
    return running


def document_of(positions, doc_lengths):
    starts = jnp.cumsum(doc_lengths) - doc_lengths
    return jnp.sum((positions[:, None] >= starts[None, :]).astype(jnp.int32), axis=1) - 1


def causal_conv(signal, rim_rows, weight, bias, positions, doc_ids, doc_lengths):
    length = signal.shape[0]
    taps = weight.shape[0]
    joined = jnp.concatenate([rim_rows, signal], axis=0).astype(jnp.float32)
    total = jnp.zeros(signal.shape, jnp.float32) + bias.astype(jnp.float32)[None, :]
    for offset in range(taps):
        lag = taps - 1 - offset
        source = document_of(positions - lag, doc_lengths)
        same = (source == doc_ids).astype(jnp.float32)
        total = (
            total
            + weight[offset].astype(jnp.float32)[None, :]
            * joined[offset : offset + length]
            * same[:, None]
        )
    return jax.nn.silu(total).astype(jnp.bfloat16)


def span_step(state, pieces, rates):
    signal, bmat, cmat, steps, doc_ids, doc_prev = pieces
    signal = signal.astype(jnp.float32)
    bmat = bmat.astype(jnp.float32)
    cmat = cmat.astype(jnp.float32)
    climb = jnp.cumsum(steps * rates[:, None], axis=1)
    extent = doc_ids.shape[0]
    order = jnp.arange(extent, dtype=jnp.int32)
    inside = (doc_ids[:, None] == doc_ids[None, :]) & (order[:, None] >= order[None, :])
    gap = climb[:, :, None] - climb[:, None, :]
    decay = jnp.where(inside[None], jnp.exp(-jnp.where(inside[None], gap, 0.0)), 0.0)
    scores = jnp.dot(cmat, bmat.T, precision=HIGH)
    weights = decay * scores[None] * steps[:, None, :]
    output = jnp.einsum("hts,shp->thp", weights, signal, precision=HIGH)
    carried = (doc_ids == doc_prev).astype(jnp.float32)
    entry = jnp.exp(-climb) * carried[None, :]
    output = output + jnp.einsum("tn,hpn->thp", cmat, state, precision=HIGH) * entry.T[:, :, None]
    last = doc_ids[extent - 1]
    tail = (
        jnp.exp(climb - climb[:, extent - 1 :])
        * (doc_ids == last).astype(jnp.float32)[None, :]
        * steps
    )
    kept = jnp.exp(-climb[:, extent - 1]) * (last == doc_prev).astype(jnp.float32)
    fresh = jnp.einsum("hs,shp,sn->hpn", tail, signal, bmat, precision=HIGH)
    return (kept[:, None, None] * state + fresh, output)


def chain_combine(earlier, later):
    return (earlier[0] * later[0], later[0][:, None, None] * earlier[1] + later[1])


def softmax_combine(first_part, second_part):
    peak = jnp.maximum(first_part[0], second_part[0])
    total = first_part[1] * jnp.exp(first_part[0] - peak) + second_part[1] * jnp.exp(
        second_part[0] - peak
    )
    return (peak, total, first_part[2] + second_part[2])


def local(
    residual,
    x_in,
    bc_in,
    z_in,
    dt_raw,
    dt_bias,
    decay_rate,
    d_skip,
    conv_x_weight,
    conv_x_bias,
    conv_bc_weight,
    conv_bc_bias,
    norm_gain,
    out_weight,
    final_gain,
    lm_weight,
    targets,
    doc_lengths,
):
    length = x_in.shape[0]
    inner_here = x_in.shape[1]
    heads_here = dt_raw.shape[0]
    seq_rank = lax.axis_index("seq")
    head_rank = lax.axis_index("head")
    offset_here = seq_rank * length
    positions = offset_here + jnp.arange(length, dtype=jnp.int32)
    doc_ids = document_of(positions, doc_lengths)
    margin = KERNEL - 1
    x_rim, bc_rim = shifted((x_in[length - margin :], bc_in[length - margin :]), "seq", 1)
    signal = causal_conv(x_in, x_rim, conv_x_weight, conv_x_bias, positions, doc_ids, doc_lengths)
    keys_queries = causal_conv(
        bc_in, bc_rim, conv_bc_weight, conv_bc_bias, positions, doc_ids, doc_lengths
    )
    steps = jax.nn.softplus(dt_raw + dt_bias[:, None])
    blocks = length // SPAN
    block_starts = offset_here + jnp.arange(blocks, dtype=jnp.int32) * SPAN
    pieces = (
        signal.reshape(blocks, SPAN, heads_here, HEAD_SIZE),
        keys_queries[:, :STATE].reshape(blocks, SPAN, STATE),
        keys_queries[:, STATE:].reshape(blocks, SPAN, STATE),
        steps.reshape(heads_here, blocks, SPAN).transpose(1, 0, 2),
        doc_ids.reshape(blocks, SPAN),
        document_of(block_starts - 1, doc_lengths),
    )

    def advance(state, piece):
        return span_step(state, piece, decay_rate)

    local_end, outputs = lax.scan(
        advance, jnp.zeros((heads_here, HEAD_SIZE, STATE), jnp.float32), pieces
    )
    outputs = outputs.reshape(length, heads_here, HEAD_SIZE)
    before = document_of(jnp.reshape(offset_here - 1, (1,)), doc_lengths)[0]
    carried = (doc_ids == before).astype(jnp.float32)
    climb = jnp.cumsum(steps * decay_rate[:, None], axis=1)
    through = jnp.exp(-climb[:, length - 1]) * carried[length - 1]
    identity = (jnp.ones_like(through), jnp.zeros_like(local_end))
    incoming = entering((through, local_end), "seq", chain_combine, identity)[1]
    entry = jnp.exp(-climb) * carried[None, :]
    cmat = keys_queries[:, STATE:].astype(jnp.float32)
    outputs = (
        outputs + jnp.einsum("tn,hpn->thp", cmat, incoming, precision=HIGH) * entry.T[:, :, None]
    )
    mixed = outputs + d_skip[None, :, None] * signal.reshape(length, heads_here, HEAD_SIZE).astype(
        jnp.float32
    )
    gated = mixed.reshape(length, inner_here) * jax.nn.silu(z_in.astype(jnp.float32))
    square_sum = lax.psum(jnp.sum(gated * gated, axis=1), "head")
    scale = lax.rsqrt(square_sum / INNER + EPSILON)
    normed = (gated * scale[:, None] * norm_gain.astype(jnp.float32)[None, :]).astype(jnp.bfloat16)
    partial_value = jnp.dot(normed, out_weight, preferred_element_type=jnp.float32)
    share = residual.shape[1]
    projected = lax.psum_scatter(partial_value, "head", scatter_dimension=1, tiled=True)
    block_out = (residual.astype(jnp.float32) + projected).astype(jnp.bfloat16)
    widened = block_out.astype(jnp.float32)
    square_total = lax.psum(jnp.sum(widened * widened, axis=1), "head")
    gain_part = lax.dynamic_slice_in_dim(final_gain, head_rank * share, share, 0)
    final_scale = lax.rsqrt(square_total / D + EPSILON)
    hidden_part = (widened * final_scale[:, None] * gain_part.astype(jnp.float32)[None, :]).astype(
        jnp.bfloat16
    )
    hidden = lax.all_gather(hidden_part, "head", axis=1, tiled=True)
    vocab_here = lm_weight.shape[1]
    logits = jnp.dot(
        hidden,
        lax.all_gather(lm_weight, "seq", axis=0, tiled=True),
        preferred_element_type=jnp.float32,
    )
    peak = jnp.max(logits, axis=1)
    total = jnp.sum(jnp.exp(logits - peak[:, None]), axis=1)
    local_target = targets - head_rank * vocab_here
    column = jnp.arange(vocab_here, dtype=jnp.int32)
    picked = jnp.sum(jnp.where(column[None, :] == local_target[:, None], logits, 0.0), axis=1)
    peak_all, total_all, picked_all = merged((peak, total, picked), "head", softmax_combine)
    losses = peak_all + jnp.log(total_all) - picked_all
    member = (
        doc_ids[:, None] == jnp.arange(doc_lengths.shape[0], dtype=jnp.int32)[None, :]
    ).astype(jnp.float32)
    sums = lax.psum(jnp.dot(losses, member, precision=HIGH), "seq")
    return (block_out, sums / doc_lengths.astype(jnp.float32))


def solution(mesh):
    in_specs = (
        P(("groups", "seq"), "head"),
        P(("groups", "seq"), "head"),
        P(("groups", "seq"), None),
        P(("groups", "seq"), "head"),
        P("head", ("groups", "seq")),
        P("head"),
        P("head"),
        P("head"),
        P(None, "head"),
        P("head"),
        P(),
        P(),
        P("head"),
        P("head", None),
        P(),
        P("seq", "head"),
        P(("groups", "seq")),
        P("groups"),
    )
    out_specs = (P(("groups", "seq"), "head"), P("groups"))
    return jax.shard_map(local, mesh=mesh, in_specs=in_specs, out_specs=out_specs, check_vma=False)
```

profile of v0, /device:TPU:0, one launch (start us, length us, event | category | flops | bytes accessed | tf_op | source)
XLA Modules:
  0.0 895.2 jit_solution(18207407152711681052)
XLA Ops:
  7.2 0.8 slice.106
  8.0 4.9 collective-permute-start
  13.7 3.5 collective-permute-start.1
  18.0 1.3 fusion.85
  20.0 0.8 slice_convert_fusion.3
  21.1 1.5 broadcast_multiply_fusion.1
  23.3 0.9 convert_reduce_fusion.7
  25.6 1.0 maximum_convert_fusion.1
  28.1 2.4 multiply_convert_fusion.1
  30.5 1.5 copy.62
  32.0 3.2 reshape.256
  35.5 83.1 %while.41 = (s32[]{:T(128)}, f32[20,64,128]{2,1,0:T(8,128)S(1)}, f32[2,256,20,64]{1,0,3,2:T(2,128)}, f32[2,20,256]{2,0,1:T(2,128)S(1)}, f32[20]{0:T(128)S(1)}, /...) while((s32[]{:T(128)}, f32[20,64,128]{2,1,0:T(8,128)S(1)}, ...), condition=%wide.region_9.10_spmd.clone, body=%wide.region_6.9_spmd.clone.sunk | while | flops 2040757376 | bytes 13968218 | solution.py:155
  37.9 1.0 fusion.117
  39.0 4.2 fusion.119
  45.4 1.3 copy.103
  46.8 27.0 %dynamic_update_slice.6 = f32[2,256,20,64]{1,0,3,2:T(2,128)} dynamic-update-slice(f32[2,256,20,64]{1,0,3,2:T(2,128)} %get-tuple-element.469, f32[1,256,20,64]{1,0,3,2:T(1,128)S(1)} %copy.103, s32[]{:T(128)} %get-tuple-element.467, s32[]{:T(128)} %constant.109.clone.1..sunk.1, s32[]{:T(128)} %constant.109.clone.1..sunk.1, s32[]{:T(128)} %constant.109.clone.1..sunk.1) | dynamic-update-slice | bytes 2621444 | tf_op jit(solution)/shard_map/while/body/jit(dynamic_update_index_in_dim)/dynamic_update_slice | solution.py:155
  75.1 1.9 fusion.116
  79.4 1.0 fusion.117
  80.5 4.2 fusion.119
  86.9 1.3 copy.103
  88.3 27.0 %dynamic_update_slice.6 = f32[2,256,20,64]{1,0,3,2:T(2,128)} dynamic-update-slice(f32[2,256,20,64]{1,0,3,2:T(2,128)} %get-tuple-element.469, f32[1,256,20,64]{1,0,3,2:T(1,128)S(1)} %copy.103, s32[]{:T(128)} %get-tuple-element.467, s32[]{:T(128)} %constant.109.clone.1..sunk.1, s32[]{:T(128)} %constant.109.clone.1..sunk.1, s32[]{:T(128)} %constant.109.clone.1..sunk.1) | dynamic-update-slice | bytes 2621444 | tf_op jit(solution)/shard_map/while/body/jit(dynamic_update_index_in_dim)/dynamic_update_slice | solution.py:155
  116.6 1.9 fusion.116
  119.4 1.3 slice.128
  121.6 1.2 reduce-window.30
  123.1 1.3 dynamic-slice
  126.1 11.2 %all-reduce = f32[80]{0:T(128)S(1)} all-reduce(f32[80]{0:T(128)S(1)} %dynamic-update-slice), channel_id=2, replica_groups=mesh['groups'=2,'seq'=4,'head'=4] {'seq'}, use_global_device_ids=true, to_apply=%add | all-reduce | flops 80 | bytes 640
  138.1 1.3 multiply_bitcast_fusion.2
  139.4 1.6 copy.68
  141.1 4.8 reshape.259
  145.8 27.9 %all-gather.16.cloned.1.call-done = f32[80,64,128]{2,1,0:T(8,128)} async-done(((f32[20,64,128]{2,1,0:T(8,128)}), f32[80,64,128]{2,1,0:T(8,128)}) %all-gather.16.cloned.1.call-update) | async-done | bytes 2621456 | tf_op jit(solution)/shard_map/all_gather | solution.py:24
  173.8 0.9 copy-done.4
  174.8 4.7 multiply_add_fusion.1
  179.4 2.1 copy.69
  181.6 2.2 multiply_reduce_fusion
  183.8 6.3 psum.21
  190.1 9.7 %fusion.63 = f32[512,2560]{1,0:T(8,128)} fusion(bf16[1280,2560]{1,0:T(8,128)(2,1)} %param.37, f32[1280]{0:T(1024)S(1)} %convert_element_type.158, f32[512]{0:T(512)S(1)} %add_rsqrt_fusion.1, f32[512,1280]{1,0:T(8,128)S(1)} %copy.69, bf16[512,1280]{1,0:T(8,128)(2,1)} %param.27), kind=kOutput, calls=%fused_computation.95 | convolution fusion | flops 3361341440 | bytes 15735808 | tf_op jit(solution)/shard_map/dot_general | solution.py:177
  200.8 51.7 %reduce-scatter.2.cloned.1.call-done = f32[512,640]{1,0:T(8,128)} async-done(((f32[512,2560]{1,0:T(8,128)}), f32[512,640]{1,0:T(8,128)}) %reduce-scatter.2.cloned.1.call-update) | async-done | bytes 1310736 | tf_op jit(solution)/shard_map/reduce_scatter | solution.py:179
  252.5 1.6 fusion.60
  254.1 5.8 psum.22
  259.8 1.1 fusion.62
  261.6 25.6 %all-gather.12.cloned.1.call-done = bf16[512,2560]{1,0:T(8,128)(2,1)} async-done(((bf16[512,640]{1,0:T(8,128)(2,1)}), bf16[512,2560]{1,0:T(8,128)(2,1)}) %all-gather.12.cloned.1.call-update) | async-done | bytes 2621456 | tf_op jit(solution)/shard_map/all_gather | solution.py:188
  287.2 550.0 %all-gather.14.cloned.1.call-done = bf16[2560,6400]{1,0:T(8,128)(2,1)} async-done(((bf16[640,6400]{1,0:T(8,128)(2,1)}), bf16[2560,6400]{1,0:T(8,128)(2,1)}) %all-gather.14.cloned.1.call-update) | async-done | bytes 32768016 | tf_op jit(solution)/shard_map/all_gather | solution.py:192
  837.2 22.0 %fusion.89 = (f32[512]{0:T(512)S(1)}, f32[512,6400]{1,0:T(8,128)S(1)}) fusion(bf16[512,2560]{1,0:T(8,128)(2,1)} %all-gather.12.cloned.1.call-done, bf16[2560,6400]{1,0:T(8,128)(2,1)} %all-gather.14.cloned.1.call-done), kind=kOutput, calls=%fused_computation.167 | convolution fusion | flops 16780492800 | bytes 48498688 | tf_op jit(solution)/shard_map/dot_general | solution.py:190
  859.3 4.0 select_reduce_fusion
  863.3 5.2 all-gather.6
  868.5 5.2 all-gather.7
  873.7 5.2 all-gather.5
  879.5 8.6 psum.23
  (154 shorter events, 21.5 us)
Async XLA Ops:
  7.2 20.6 %copy-start.5 = (bf16[512,1280]{1,0:T(8,128)(2,1)S(1)}, bf16[512,1280]{1,0:T(8,128)(2,1)}, u32[]{:S(2)}) copy-start(bf16[512,1280]{1,0:T(8,128)(2,1)} %param.25) | copy-start | bytes 3932164
  7.2 166.6 %all-gather.16.cloned.1.call-start = ((), (), s32[]{:S(2)}) async-start(), calls=%async_computation.4 | async-start | bytes 3276800 | tf_op jit(solution)/shard_map/all_gather | solution.py:24
  8.0 19.7 %collective-permute-start = (bf16[3,1280]{1,0:T(4,128)(2,1)S(1)}, bf16[3,1280]{1,0:T(4,128)(2,1)S(1)}, u32[]{:S(2)}, u32[]{:S(2)}) collective-permute-start(bf16[3,1280]{1,0:T(4,128)(2,1)S(1)} %slice.106), channel_id=1, source_target_pairs={{0,4},{4,8},{8,12},{1,5},{5,9},{9,13},{2,6},{6,10},{10,14},{3,7},{... | collective-permute-start | bytes 23048 | tf_op jit(solution)/shard_map/ppermute | solution.py:19
  13.7 11.9 %collective-permute-start.1 = (bf16[3,256]{1,0:T(4,128)(2,1)S(1)}, bf16[3,256]{1,0:T(4,128)(2,1)S(1)}, u32[]{:S(2)}, u32[]{:S(2)}) collective-permute-start(bf16[3,256]{1,0:T(4,128)(2,1)S(1)} %slice.115), channel_id=1, source_target_pairs={{0,4},{4,8},{8,12},{1,5},{5,9},{9,13},{2,6},{6,10},{10,14},{3,7},{... | collective-permute-start | bytes 4616 | tf_op jit(solution)/shard_map/ppermute | solution.py:19
  20.9 7.1 copy-start.9
  27.0 1.0 copy-start.3
  30.5 1.5 copy-start.1
  32.0 3.4 copy-start.7
  35.5 3.5 copy-start.14
  46.7 30.2 %copy-start.8 = (f32[20]{0:T(128)S(1)}, f32[20]{0:T(128)}, u32[]{:S(2)}) copy-start(f32[20]{0:T(128)} %get-tuple-element.571) | copy-start | bytes 244 | tf_op jit(solution)/shard_map/while
  46.7 30.2 %copy-start.15 = (s32[2]{0:T(128)S(1)}, s32[2]{0:T(128)}, u32[]{:S(2)}) copy-start(s32[2]{0:T(128)} %copy-done.14) | copy-start | bytes 28 | tf_op jit(solution)/shard_map/while
  77.0 3.5 copy-start.14
  88.3 30.2 %copy-start.8 = (f32[20]{0:T(128)S(1)}, f32[20]{0:T(128)}, u32[]{:S(2)}) copy-start(f32[20]{0:T(128)} %get-tuple-element.571) | copy-start | bytes 244 | tf_op jit(solution)/shard_map/while
  88.3 30.2 %copy-start.15 = (s32[2]{0:T(128)S(1)}, s32[2]{0:T(128)}, u32[]{:S(2)}) copy-start(s32[2]{0:T(128)} %copy-done.14) | copy-start | bytes 28 | tf_op jit(solution)/shard_map/while
  118.5 0.8 copy-start
  119.4 133.1 %reduce-scatter.2.cloned.1.call-start = ((), (), s32[]{:S(2)}) async-start(), calls=%async_computation.1 | async-start | bytes 6553600 | tf_op jit(solution)/shard_map/reduce_scatter | solution.py:179
  173.8 1.0 copy-start.4
  173.8 0.9 copy-start.12
  199.9 52.6 %copy-start.6 = (bf16[512,640]{1,0:T(8,128)(2,1)S(1)}, bf16[512,640]{1,0:T(8,128)(2,1)}, u32[]{:S(2)}) copy-start(bf16[512,640]{1,0:T(8,128)(2,1)} %param.24) | copy-start | bytes 1966084
  199.9 87.4 %all-gather.12.cloned.1.call-start = ((), (), s32[]{:S(2)}) async-start(), calls=%async_computation.2 | async-start | bytes 3276800 | tf_op jit(solution)/shard_map/all_gather | solution.py:188
  254.1 7.5 copy-start.2
  260.9 0.7 copy-start.11
  260.9 576.3 %all-gather.14.cloned.1.call-start = ((), (), s32[]{:S(2)}) async-start(), calls=%async_computation.3 | async-start | bytes 40960000 | tf_op jit(solution)/shard_map/all_gather | solution.py:192
  859.3 19.9 %copy-start.10 = (s32[512]{0:T(512)S(1)}, s32[512]{0:T(512)}, u32[]{:S(2)}) copy-start(s32[512]{0:T(512)} %copy-done.9) | copy-start | bytes 6148
  859.3 28.8 %copy-start.13 = (s32[4]{0:T(128)S(1)}, s32[4]{0:T(128)}, u32[]{:S(2)}) copy-start(s32[4]{0:T(128)} %param.41) | copy-start | bytes 52
Sparse Core Ops, SparseCore 0:
  119.5 54.1 all-gather.15
  200.0 52.4 reduce-scatter.1
  261.1 26.1 all-gather.11
  288.7 548.5 all-gather.13
where the time goes:
time: 900 us; the launch traced here: 895 us
  waiting for transfers between devices  656 us (73%)
  local copies, waits for them, and re-layouts  81.8 us (9%)
  matrix products  52.3 us (6%)
  blocking collectives  47.5 us (5%)
  other arithmetic  30.7 us (3%)
  between operations  15.5 us (2%)
    all_gather x1, waiting for transfers between devices, local(): lax.all_gather(lm_weight, 'seq', axis=0, tiled=True)  550 us
    dynamic_update_slice x4, local copies, waits for them, and re-layouts, local(): lax.scan(advance, jnp.zeros((heads_here, HEAD_SIZE, STATE), jnp.float32),...  56.8 us
    reduce_scatter x1, waiting for transfers between devices, local(): lax.psum_scatter(partial_value, 'head', scatter_dimension=1, tiled=True)  51.7 us
    all_gather x1, waiting for transfers between devices, entering(): gathered = jax.tree.map(lambda a: lax.all_gather(a, axis), part)  27.9 us
    all_gather x1, waiting for transfers between devices, local(): hidden = lax.all_gather(hidden_part, 'head', axis=1, tiled=True)  25.6 us
    dot_general x1, matrix products, local(): jnp.dot(hidden, lax.all_gather(lm_weight, 'seq', axis=0, tiled=True), pre...  22 us
  transfers between devices with their start and end apart: 6, of which 4 were waited for; matrix products, arithmetic and copies ran while one was open for 3% of the time, Pallas kernels for 0%

commit v1 on v0

--- a/solution.py
+++ b/solution.py
@@ -189,7 +189,9 @@
     vocab_here = lm_weight.shape[1]
     logits = jnp.dot(
         hidden,
-        lax.all_gather(lm_weight, "seq", axis=0, tiled=True),
+        jnp.concatenate(
+            lax.all_to_all(jnp.stack([lm_weight] * lax.axis_size("seq")), "seq", 0, 0), axis=0
+        ),
         preferred_element_type=jnp.float32,
     )
     peak = jnp.max(logits, axis=1)

time: 900 us -> 1070 us (1.19)
  blocking collectives: 47.5 us -> 226 us
  waiting for transfers between devices: 656 us -> 624 us
  local copies, waits for them, and re-layouts: 81.8 us -> 94.5 us
    all_gather x1 -> x0, waiting for transfers between devices: 550 us -> none  [local(): lax.all_gather(lm_weight, 'seq', axis=0, tiled=True)]
    ppermute x2, waiting for transfers between devices: 0.01 us -> 515 us  [shifted(): return lax.ppermute(array, axis, pairs)]
    unnamed x1, blocking collectives: 11.2 us -> 187 us
    another operation x10 -> x11, local copies, waits for them, and re-layouts: 1.11 us -> 14.3 us  [the longest x1 13.1 us: local(): jnp.stack([lm_weight] * lax.axis_size('seq'))]
  transfers between devices with their start and end apart: 6 -> 6, of which waited for: 4 -> 4; matrix products, arithmetic and copies ran while one was open for 3% -> 12% of each run, Pallas kernels for 0% -> 0%
where the time goes in v1:
time: 1070 us; the launch traced here: 1060 us
  waiting for transfers between devices  624 us (58%)
  blocking collectives  226 us (21%)
  local copies, waits for them, and re-layouts  94.5 us (9%)
  matrix products  52.3 us (5%)
  other arithmetic  27.1 us (3%)
  starting transfers between devices  18.3 us (2%)
  between operations  15.6 us (1%)
    ppermute x2, waiting for transfers between devices, shifted(): return lax.ppermute(array, axis, pairs)  515 us
    unnamed x1, blocking collectives  187 us
    dynamic_update_slice x4, local copies, waits for them, and re-layouts, local(): lax.scan(advance, jnp.zeros((heads_here, HEAD_SIZE, STATE), jnp.float32),...  56.8 us
    reduce_scatter x1, waiting for transfers between devices, local(): lax.psum_scatter(partial_value, 'head', scatter_dimension=1, tiled=True)  51.6 us
    all_gather x1, waiting for transfers between devices, entering(): gathered = jax.tree.map(lambda a: lax.all_gather(a, axis), part)  31 us
    all_gather x1, waiting for transfers between devices, local(): hidden = lax.all_gather(hidden_part, 'head', axis=1, tiled=True)  26.3 us
    dot_general x1, matrix products, local(): jnp.dot(hidden, jnp.concatenate(lax.all_to_all(jnp.stack([lm_weight] * la...  22 us
  transfers between devices with their start and end apart: 6, of which 4 were waited for; matrix products, arithmetic and copies ran while one was open for 12% of the time, Pallas kernels for 0%

profile of v1, /device:TPU:0, one launch (start us, length us, event | category | flops | bytes accessed | tf_op | source)
XLA Modules:
  0.0 1060.7 jit_solution(8223033496674715499)
XLA Ops:
  7.2 13.1 %stack.2 = bf16[4,640,6400]{2,1,0:T(8,128)(2,1)} broadcast(bf16[640,6400]{1,0:T(8,128)(2,1)} %param.39), dimensions={1,2} | broadcast | bytes 40960000 | tf_op jit(solution)/shard_map/stack | solution.py:193
  20.4 9.7 all-to-all-start
  30.2 5.0 collective-permute-start
  35.2 3.5 collective-permute-start.1
  41.7 1.4 broadcast_multiply_fusion.1
  43.2 514.9 %collective-permute-done.1 = bf16[3,256]{1,0:T(4,128)(2,1)S(1)} collective-permute-done((bf16[3,256]{1,0:T(4,128)(2,1)S(1)}, bf16[3,256]{1,0:T(4,128)(2,1)S(1)}, u32[]{:S(2)}, u32[]{:S(2)}) %collective-permute-start.1) | collective-permute-done | bytes 1568 | tf_op jit(solution)/shard_map/ppermute | solution.py:19
  559.7 2.6 multiply_convert_fusion.1
  562.3 1.5 copy.62
  563.8 3.2 reshape.261
  567.2 85.5 %while.41 = (s32[]{:T(128)}, f32[20,64,128]{2,1,0:T(8,128)S(1)}, f32[2,256,20,64]{1,0,3,2:T(2,128)}, f32[2,20,256]{2,0,1:T(2,128)S(1)}, f32[20]{0:T(128)}, /*ind...) while((s32[]{:T(128)}, f32[20,64,128]{2,1,0:T(8,128)S(1)}, ...), condition=%wide.region_9.10_spmd.clone, body=%wide.region_6.9_spmd.clone.sunk | while | flops 2040757376 | bytes 13967742 | solution.py:155
  568.9 1.2 dynamic_slice.109
  570.8 1.0 fusion.117
  571.9 4.2 fusion.119
  578.4 1.3 copy.103
  579.8 27.0 %dynamic_update_slice.6 = f32[2,256,20,64]{1,0,3,2:T(2,128)} dynamic-update-slice(f32[2,256,20,64]{1,0,3,2:T(2,128)} %get-tuple-element.469, f32[1,256,20,64]{1,0,3,2:T(1,128)S(1)} %copy.103, s32[]{:T(128)} %get-tuple-element.467, s32[]{:T(128)} %constant.109.clone.1..sunk.1, s32[]{:T(128)} %constant.109.clone.1..sunk.1, s32[]{:T(128)} %constant.109.clone.1..sunk.1) | dynamic-update-slice | bytes 2621444 | tf_op jit(solution)/shard_map/while/body/jit(dynamic_update_index_in_dim)/dynamic_update_slice | solution.py:155
  608.0 1.9 fusion.116
  611.7 1.2 dynamic_slice.109
  613.6 1.0 fusion.117
  614.6 4.2 fusion.119
  621.1 1.3 copy.103
  622.5 27.0 %dynamic_update_slice.6 = f32[2,256,20,64]{1,0,3,2:T(2,128)} dynamic-update-slice(f32[2,256,20,64]{1,0,3,2:T(2,128)} %get-tuple-element.469, f32[1,256,20,64]{1,0,3,2:T(1,128)S(1)} %copy.103, s32[]{:T(128)} %get-tuple-element.467, s32[]{:T(128)} %constant.109.clone.1..sunk.1, s32[]{:T(128)} %constant.109.clone.1..sunk.1, s32[]{:T(128)} %constant.109.clone.1..sunk.1) | dynamic-update-slice | bytes 2621444 | tf_op jit(solution)/shard_map/while/body/jit(dynamic_update_index_in_dim)/dynamic_update_slice | solution.py:155
  650.8 1.9 fusion.116
  652.7 0.8 copy-done
  653.6 1.2 slice.128
  655.7 1.2 reduce-window.30
  657.2 1.3 dynamic-slice
  660.1 186.7 %all-reduce = f32[80]{0:T(128)S(1)} all-reduce(f32[80]{0:T(128)S(1)} %dynamic-update-slice), channel_id=2, replica_groups=mesh['groups'=2,'seq'=4,'head'=4] {'seq'}, use_global_device_ids=true, to_apply=%add | all-reduce | flops 80 | bytes 640
  847.6 1.3 multiply_bitcast_fusion.2
  848.9 1.6 copy.68
  850.5 4.7 reshape.264
  855.2 31.0 %all-gather.13.cloned.1.call-done = f32[80,64,128]{2,1,0:T(8,128)} async-done(((f32[20,64,128]{2,1,0:T(8,128)}), f32[80,64,128]{2,1,0:T(8,128)}) %all-gather.13.cloned.1.call-update) | async-done | bytes 2621456 | tf_op jit(solution)/shard_map/all_gather | solution.py:24
  886.3 0.9 copy-done.4
  887.3 4.7 multiply_add_fusion.1
  891.9 2.1 copy.69
  894.1 2.2 multiply_reduce_fusion
  896.3 6.4 psum.21
  902.7 9.7 fusion.63
  913.3 51.6 %reduce-scatter.2.cloned.1.call-done = f32[512,640]{1,0:T(8,128)} async-done(((f32[512,2560]{1,0:T(8,128)}), f32[512,640]{1,0:T(8,128)}) %reduce-scatter.2.cloned.1.call-update) | async-done | bytes 1310736 | tf_op jit(solution)/shard_map/reduce_scatter | solution.py:179
  964.9 1.6 fusion.60
  966.5 5.8 psum.22
  972.3 1.1 fusion.62
  973.4 26.3 %all-gather.11.cloned.1.call-done = bf16[512,2560]{1,0:T(8,128)(2,1)} async-done(((bf16[512,640]{1,0:T(8,128)(2,1)}), bf16[512,2560]{1,0:T(8,128)(2,1)}) %all-gather.11.cloned.1.call-update) | async-done | bytes 2621456 | tf_op jit(solution)/shard_map/all_gather | solution.py:188
  999.7 22.0 %fusion.89 = (f32[512]{0:T(512)S(1)}, f32[512,6400]{1,0:T(8,128)S(1)}) fusion(bf16[512,2560]{1,0:T(8,128)(2,1)} %all-gather.11.cloned.1.call-done, bf16[2560,6400]{1,0:T(8,128)(2,1)} %bitcast.21), kind=kOutput, calls=%fused_computation.167 | convolution fusion | flops 16780492800 | bytes 48498688 | tf_op jit(solution)/shard_map/dot_general | solution.py:190
  1021.8 4.0 select_reduce_fusion
  1025.8 5.2 all-gather.6
  1031.0 5.2 all-gather.7
  1036.2 5.2 all-gather.5
  1041.9 11.7 %psum.23 = f32[4]{0:T(128)S(1)} all-reduce(f32[4]{0:T(128)S(1)} %convolution_bitcast_fusion), channel_id=1, replica_groups=mesh['groups'=2,'seq'=4,'head'=4] {'seq'}, use_global_device_ids=true, to_apply=%region_25.26 | all-reduce | flops 4 | bytes 32 | tf_op jit(solution)/shard_map/psum | solution.py:207
  (156 shorter events, 18.8 us)
Async XLA Ops:
  20.3 9.9 copy-start.5
  20.3 14.9 %copy-start.7 = (bf16[512,256]{1,0:T(8,128)(2,1)S(1)}, bf16[512,256]{1,0:T(8,128)(2,1)}, u32[]{:S(2)}) copy-start(bf16[512,256]{1,0:T(8,128)(2,1)} %param.26) | copy-start | bytes 786436
  20.3 18.4 %copy-start.17 = (s32[4]{0:T(128)S(1)}, s32[4]{0:T(128)}, u32[]{:S(2)}) copy-start(s32[4]{0:T(128)} %param.41) | copy-start | bytes 52
  20.3 20.8 %copy-start.10 = (bf16[4,256]{1,0:T(4,128)(2,1)S(1)}, bf16[4,256]{1,0:T(4,128)(2,1)}, u32[]{:S(2)}) copy-start(bf16[4,256]{1,0:T(4,128)(2,1)} %param.34) | copy-start | bytes 6148
  20.3 21.4 %copy-start.8 = (f32[20,512]{1,0:T(8,128)S(1)}, f32[20,512]{1,0:T(8,128)}, u32[]{:S(2)}) copy-start(f32[20,512]{1,0:T(8,128)} %param.28) | copy-start | bytes 122884
  20.3 21.4 %copy-start.15 = (f32[20]{0:T(128)S(1)}, f32[20]{0:T(128)}, u32[]{:S(2)}) copy-start(f32[20]{0:T(128)} %param.29) | copy-start | bytes 244
  20.4 22.7 %copy-start.9 = (bf16[4,1280]{1,0:T(4,128)(2,1)S(1)}, bf16[4,1280]{1,0:T(4,128)(2,1)}, u32[]{:S(2)}) copy-start(bf16[4,1280]{1,0:T(4,128)(2,1)} %param.32) | copy-start | bytes 30724
  20.4 22.8 %copy-start.13 = (bf16[1280]{0:T(1024)(128)(2,1)S(1)}, bf16[1280]{0:T(1024)(128)(2,1)}, u32[]{:S(2)}) copy-start(bf16[1280]{0:T(1024)(128)(2,1)} %param.33) | copy-start | bytes 7684
  20.4 22.8 %copy-start.19 = (bf16[256]{0:T(256)(128)(2,1)S(1)}, bf16[256]{0:T(256)(128)(2,1)}, u32[]{:S(2)}) copy-start(bf16[256]{0:T(256)(128)(2,1)} %param.35) | copy-start | bytes 1540
  20.4 979.3 %all-to-all-start = ((bf16[4,640,6400]{2,1,0:T(8,128)(2,1)}), bf16[4,640,6400]{2,1,0:T(8,128)(2,1)}, u32[]{:S(2)}, u32[]{:S(2)}) async-start(bf16[4,640,6400]{2,1,0:T(8,128)(2,1)} %stack.2), calls=%async_computation.1 | async-start | bytes 65536000 | tf_op jit(solution)/shard_map/all_to_all | solution.py:193
  30.1 856.1 %all-gather.13.cloned.1.call-start = ((), (), s32[]{:S(2)}) async-start(), calls=%async_computation.4 | async-start | bytes 3276800 | tf_op jit(solution)/shard_map/all_gather | solution.py:24
  30.2 529.2 %collective-permute-start = (bf16[3,1280]{1,0:T(4,128)(2,1)S(1)}, bf16[3,1280]{1,0:T(4,128)(2,1)S(1)}, u32[]{:S(2)}, u32[]{:S(2)}) collective-permute-start(bf16[3,1280]{1,0:T(4,128)(2,1)S(1)} %slice.106), channel_id=1, source_target_pairs={{0,4},{4,8},{8,12},{1,5},{5,9},{9,13},{2,6},{6,10},{10,14},{3,7},{... | collective-permute-start | bytes 23048 | tf_op jit(solution)/shard_map/ppermute | solution.py:19
  35.2 522.9 %collective-permute-start.1 = (bf16[3,256]{1,0:T(4,128)(2,1)S(1)}, bf16[3,256]{1,0:T(4,128)(2,1)S(1)}, u32[]{:S(2)}, u32[]{:S(2)}) collective-permute-start(bf16[3,256]{1,0:T(4,128)(2,1)S(1)} %slice.115), channel_id=1, source_target_pairs={{0,4},{4,8},{8,12},{1,5},{5,9},{9,13},{2,6},{6,10},{10,14},{3,7},{... | collective-permute-start | bytes 4616 | tf_op jit(solution)/shard_map/ppermute | solution.py:19
  41.1 518.6 %copy-start.11 = (s32[512]{0:T(512)}, s32[512]{0:T(512)S(1)}, u32[]{:S(2)}) copy-start(s32[512]{0:T(512)S(1)} %broadcast_add_fusion.2) | copy-start | bytes 6148
  558.6 1.0 copy-start.3
  562.3 1.5 copy-start.1
  652.7 0.8 copy-start
  653.6 311.4 %reduce-scatter.2.cloned.1.call-start = ((), (), s32[]{:S(2)}) async-start(), calls=%async_computation.2 | async-start | bytes 6553600 | tf_op jit(solution)/shard_map/reduce_scatter | solution.py:179
  886.3 1.0 copy-start.4
  886.3 0.9 copy-start.16
  912.4 52.5 %copy-start.6 = (bf16[512,640]{1,0:T(8,128)(2,1)S(1)}, bf16[512,640]{1,0:T(8,128)(2,1)}, u32[]{:S(2)}) copy-start(bf16[512,640]{1,0:T(8,128)(2,1)} %param.24) | copy-start | bytes 1966084
  912.5 61.0 %copy-start.14 = (s32[512]{0:T(512)S(1)}, s32[512]{0:T(512)}, u32[]{:S(2)}) copy-start(s32[512]{0:T(512)} %param.40) | copy-start | bytes 6148
  912.5 87.3 %all-gather.11.cloned.1.call-start = ((), (), s32[]{:S(2)}) async-start(), calls=%async_computation.3 | async-start | bytes 3276800 | tf_op jit(solution)/shard_map/all_gather | solution.py:188
  966.5 55.2 %copy-start.2 = (bf16[512,640]{1,0:T(8,128)(2,1)}, bf16[512,640]{1,0:T(8,128)(2,1)S(1)}, u32[]{:S(2)}) copy-start(bf16[512,640]{1,0:T(8,128)(2,1)S(1)} %get-tuple-element.276) | copy-start | bytes 1966084
  1021.7 19.9 %copy-start.12 = (s32[512]{0:T(512)S(1)}, s32[512]{0:T(512)}, u32[]{:S(2)}) copy-start(s32[512]{0:T(512)} %copy-done.11) | copy-start | bytes 6148
  1021.7 31.9 %copy-start.18 = (s32[4]{0:T(128)S(1)}, s32[4]{0:T(128)}, u32[]{:S(2)}) copy-start(s32[4]{0:T(128)} %param.41) | copy-start | bytes 52
Sparse Core Ops, SparseCore 0:
  653.7 232.5 all-gather.12
  912.6 52.3 reduce-scatter.1
  973.5 26.1 all-gather.10
